TPU v7x, 8 devices: a whole 2x2x1 slice. The times are simulated.
8 devices in a mesh: b: 1 (over z), rep: 2 (over y), col: 2 (over x), row: 2 (over core).
Axes of the slice: x: 2, y: 2, z: 1, core: 2. Of those that a mesh axis runs over, the one named last changes fastest.
Arguments:
- a_blocks: float32 [64, 64, 128, 128], P(('b', 'row'), 'col')
Outputs:
- output: float32 [64, 64, 128, 128], P(('b', 'row'), 'col')
All inputs are finite; a program needn't handle non-finite values.
Results may differ from a plain program's by a relative error of at most 0.001.
Values sent between devices are 32-bit elements.
A program may use at most 1 GiB of HBM per device.

v0:
```python
import jax
import jax.numpy as jnp
from jax import lax
from jax.sharding import PartitionSpec as P


def solution(mesh):
    row_size = mesh.shape["row"]
    col_size = mesh.shape["col"]
    rep_size = mesh.shape["rep"]
    grid_spec = P(("b", "row"), "col")

    def local_factor(a_loc):
        rows_blk, cols_blk, blk_size, _ = a_loc.shape
        num_steps = rows_blk * row_size
        share_len = blk_size // rep_size
        row_idx = lax.axis_index("row")
        col_idx = lax.axis_index("col")
        rep_idx = lax.axis_index("rep")
        work_mat = jnp.where(rep_idx == 0, a_loc, 0.0)
        out_cols = [jnp.zeros((rows_blk, blk_size, blk_size), jnp.float32)] * cols_blk
        for step_idx in range(num_steps):
            step_row = step_idx % row_size
            step_col = step_idx % col_size
            first_row = step_idx // row_size
            first_col = step_idx // col_size
            tail_rows = rows_blk - first_row
            col_sum = lax.psum(work_mat[first_row:, first_col], "rep")
            diag_mine = jnp.where(row_idx == step_row, col_sum[0], 0.0)
            diag_fac = jnp.tril(jnp.linalg.cholesky(lax.psum(diag_mine, "row")))
            solved = lax.linalg.triangular_solve(
                diag_fac, col_sum.reshape(tail_rows * blk_size, blk_size),
                left_side=False, lower=True, transpose_a=True,
            ).reshape(tail_rows, blk_size, blk_size)
            glob_row = ((first_row + jnp.arange(tail_rows)) * row_size + row_idx)[:, None, None]
            panel_blk = jnp.where(glob_row > step_idx, solved, jnp.where(glob_row == step_idx, diag_fac, 0.0))
            is_owner = col_idx == step_col
            padded = jnp.pad(panel_blk, ((first_row, 0), (0, 0), (0, 0)))
            out_cols[first_col] = jnp.where(is_owner, padded, out_cols[first_col])
            if step_idx < num_steps - 1:
                panel_row = lax.psum(jnp.where(is_owner, panel_blk, 0.0), "col")
                gathered = lax.all_gather(panel_row, "row", axis=1)
                col_full = jnp.pad(
                    gathered.reshape(tail_rows * row_size, blk_size, blk_size),
                    ((first_row * row_size, 0), (0, 0), (0, 0)),
                )
                col_grid = col_full.reshape(cols_blk, col_size, blk_size, blk_size)[first_col:]
                panel_col = lax.dynamic_index_in_dim(col_grid, col_idx, axis=1, keepdims=False)
                row_share = lax.dynamic_slice_in_dim(panel_row, rep_idx * share_len, share_len, axis=2)
                col_share = lax.dynamic_slice_in_dim(panel_col, rep_idx * share_len, share_len, axis=2)
                update = jnp.einsum(
                    "tak,uck->tuac", row_share, col_share,
                    precision=lax.Precision.HIGHEST, preferred_element_type=jnp.float32,
                )
                trail_new = work_mat[first_row:, first_col:] - update
                work_mat = lax.dynamic_update_slice(work_mat, trail_new, (first_row, first_col, 0, 0))
        return jnp.stack(out_cols, axis=1)

    return jax.shard_map(local_factor, mesh=mesh, in_specs=grid_spec, out_specs=grid_spec, check_vma=False)
```

profile of v0, /device:TPU:0, one launch (start us, length us, event | category | flops | bytes accessed | tf_op | source)
XLA Modules:
  0.0 9870.9 jit_solution(5687707343530171305)
XLA Ops:
  53.8 60.0 all-reduce.254.cloned.1.call-done
  161.9 58.4 all-reduce.258.cloned.1.call-done
  232.9 61.6 bitcast_subtract_fusion.1
  297.7 58.4 all-reduce.260.cloned.1.call-done
  403.8 58.4 all-reduce.264.cloned.1.call-done
  475.0 61.6 bitcast_subtract_fusion
  539.8 57.0 all-reduce.266.cloned.1.call-done
  645.2 57.0 all-reduce.270.cloned.1.call-done
  714.6 58.5 slice_subtract_fusion
  776.3 57.0 all-reduce.272.cloned.1.call-done
  881.6 57.0 all-reduce.276.cloned.1.call-done
  951.0 58.6 bitcast_subtract_fusion.2
  1012.7 55.5 all-reduce.278.cloned.1.call-done
  1116.3 55.6 all-reduce.282.cloned.1.call-done
  1184.1 56.2 slice_subtract_fusion.1
  1243.3 55.5 all-reduce.284.cloned.1.call-done
  1347.0 55.6 all-reduce.288.cloned.1.call-done
  1414.8 56.2 bitcast_subtract_fusion.3
  1474.1 54.1 all-reduce.290.cloned.1.call-done
  1576.5 54.1 all-reduce.294.cloned.1.call-done
  1642.8 57.4 slice_subtract_fusion.2
  1703.2 54.1 all-reduce.296.cloned.1.call-done
  1805.6 54.1 all-reduce.300.cloned.1.call-done
  1871.9 57.4 bitcast_subtract_fusion.4
  1932.3 52.7 all-reduce.302.cloned.1.call-done
  2032.8 52.7 all-reduce.306.cloned.1.call-done
  2097.3 51.2 slice_subtract_fusion.3
  2151.5 52.7 all-reduce.308.cloned.1.call-done
  2252.0 52.7 all-reduce.312.cloned.1.call-done
  2316.6 51.5 bitcast_subtract_fusion.5
  2371.1 51.2 all-reduce.314.cloned.1.call-done
  2469.6 51.3 all-reduce.318.cloned.1.call-done
  2532.6 45.6 slice_subtract_fusion.4
  2581.2 51.3 all-reduce.320.cloned.1.call-done
  2679.5 51.3 all-reduce.324.cloned.1.call-done
  2742.3 45.6 bitcast_subtract_fusion.6
  2790.8 49.8 all-reduce.326.cloned.1.call-done
  2885.9 49.9 all-reduce.330.cloned.1.call-done
  2994.5 49.8 all-reduce.332.cloned.1.call-done
  3089.4 49.9 all-reduce.336.cloned.1.call-done
  3198.0 48.4 all-reduce.338.cloned.1.call-done
  3291.5 48.4 all-reduce.342.cloned.1.call-done
  3398.0 48.4 all-reduce.344.cloned.1.call-done
  3491.7 48.4 all-reduce.348.cloned.1.call-done
  3598.0 47.0 all-reduce.350.cloned.1.call-done
  3689.4 47.0 all-reduce.354.cloned.1.call-done
  3787.6 47.0 all-reduce.356.cloned.1.call-done
  3879.0 47.0 all-reduce.360.cloned.1.call-done
  (1963 shorter events, 7288.5 us)
Async XLA Ops:
  6.5 107.3 %all-reduce.254.cloned.1.call-start = ((), (), s32[]{:S(2)}) async-start(), calls=%async_computation | async-start | bytes 4194304 | tf_op jit(solution)/shard_map/psum | solution.py:28
  115.3 104.9 %all-reduce.258.cloned.1.call-start = ((), (), s32[]{:S(2)}) async-start(), calls=%async_computation.2 | async-start | bytes 4194304 | tf_op jit(solution)/shard_map/psum | solution.py:41
  220.3 135.8 %all-reduce.260.cloned.1.call-start = ((), (), s32[]{:S(2)}) async-start(), calls=%async_computation.3 | async-start | bytes 4194304 | tf_op jit(solution)/shard_map/psum | solution.py:28
  357.6 104.6 %all-reduce.264.cloned.1.call-start = ((), (), s32[]{:S(2)}) async-start(), calls=%async_computation.5 | async-start | bytes 4194304 | tf_op jit(solution)/shard_map/psum | solution.py:41
  462.3 134.5 %all-reduce.266.cloned.1.call-start = ((), (), s32[]{:S(2)}) async-start(), calls=%async_computation.6 | async-start | bytes 4063232 | tf_op jit(solution)/shard_map/psum | solution.py:28
  598.3 103.9 %all-reduce.270.cloned.1.call-start = ((), (), s32[]{:S(2)}) async-start(), calls=%async_computation.8 | async-start | bytes 4063232 | tf_op jit(solution)/shard_map/psum | solution.py:41
  702.2 131.1 %all-reduce.272.cloned.1.call-start = ((), (), s32[]{:S(2)}) async-start(), calls=%async_computation.9 | async-start | bytes 4063232 | tf_op jit(solution)/shard_map/psum | solution.py:28
  834.8 103.8 %all-reduce.276.cloned.1.call-start = ((), (), s32[]{:S(2)}) async-start(), calls=%async_computation.11 | async-start | bytes 4063232 | tf_op jit(solution)/shard_map/psum | solution.py:41
  938.6 129.7 %all-reduce.278.cloned.1.call-start = ((), (), s32[]{:S(2)}) async-start(), calls=%async_computation.12 | async-start | bytes 3932160 | tf_op jit(solution)/shard_map/psum | solution.py:28
  1069.8 102.1 %all-reduce.282.cloned.1.call-start = ((), (), s32[]{:S(2)}) async-start(), calls=%async_computation.14 | async-start | bytes 3932160 | tf_op jit(solution)/shard_map/psum | solution.py:41
  1171.9 127.0 %all-reduce.284.cloned.1.call-start = ((), (), s32[]{:S(2)}) async-start(), calls=%async_computation.15 | async-start | bytes 3932160 | tf_op jit(solution)/shard_map/psum | solution.py:28
  1300.3 102.2 %all-reduce.288.cloned.1.call-start = ((), (), s32[]{:S(2)}) async-start(), calls=%async_computation.17 | async-start | bytes 3932160 | tf_op jit(solution)/shard_map/psum | solution.py:41
  1402.6 125.6 %all-reduce.290.cloned.1.call-start = ((), (), s32[]{:S(2)}) async-start(), calls=%async_computation.18 | async-start | bytes 3801088 | tf_op jit(solution)/shard_map/psum | solution.py:28
  1529.7 101.0 %all-reduce.294.cloned.1.call-start = ((), (), s32[]{:S(2)}) async-start(), calls=%async_computation.20 | async-start | bytes 3801088 | tf_op jit(solution)/shard_map/psum | solution.py:41
  1630.7 126.6 %all-reduce.296.cloned.1.call-start = ((), (), s32[]{:S(2)}) async-start(), calls=%async_computation.21 | async-start | bytes 3801088 | tf_op jit(solution)/shard_map/psum | solution.py:28
  1758.8 100.9 %all-reduce.300.cloned.1.call-start = ((), (), s32[]{:S(2)}) async-start(), calls=%async_computation.23 | async-start | bytes 3801088 | tf_op jit(solution)/shard_map/psum | solution.py:41
  1859.7 125.3 %all-reduce.302.cloned.1.call-start = ((), (), s32[]{:S(2)}) async-start(), calls=%async_computation.24 | async-start | bytes 3670016 | tf_op jit(solution)/shard_map/psum | solution.py:28
  1986.5 99.0 %all-reduce.306.cloned.1.call-start = ((), (), s32[]{:S(2)}) async-start(), calls=%async_computation.26 | async-start | bytes 3670016 | tf_op jit(solution)/shard_map/psum | solution.py:41
  2085.5 118.7 %all-reduce.308.cloned.1.call-start = ((), (), s32[]{:S(2)}) async-start(), calls=%async_computation.27 | async-start | bytes 3670016 | tf_op jit(solution)/shard_map/psum | solution.py:28
  2205.7 99.0 %all-reduce.312.cloned.1.call-start = ((), (), s32[]{:S(2)}) async-start(), calls=%async_computation.29 | async-start | bytes 3670016 | tf_op jit(solution)/shard_map/psum | solution.py:41
  2304.7 117.6 %all-reduce.314.cloned.1.call-start = ((), (), s32[]{:S(2)}) async-start(), calls=%async_computation.30 | async-start | bytes 3538944 | tf_op jit(solution)/shard_map/psum | solution.py:28
  2423.8 97.1 all-reduce.318.cloned.1.call-start
  2520.9 111.6 %all-reduce.320.cloned.1.call-start = ((), (), s32[]{:S(2)}) async-start(), calls=%async_computation.33 | async-start | bytes 3538944 | tf_op jit(solution)/shard_map/psum | solution.py:28
  2634.0 96.8 all-reduce.324.cloned.1.call-start
  2730.8 109.9 %all-reduce.326.cloned.1.call-start = ((), (), s32[]{:S(2)}) async-start(), calls=%async_computation.36 | async-start | bytes 3407872 | tf_op jit(solution)/shard_map/psum | solution.py:28
  2842.2 93.6 all-reduce.330.cloned.1.call-start
  2935.8 108.6 %all-reduce.332.cloned.1.call-start = ((), (), s32[]{:S(2)}) async-start(), calls=%async_computation.39 | async-start | bytes 3407872 | tf_op jit(solution)/shard_map/psum | solution.py:28
  3045.8 93.5 all-reduce.336.cloned.1.call-start
  3139.3 107.1 %all-reduce.338.cloned.1.call-start = ((), (), s32[]{:S(2)}) async-start(), calls=%async_computation.42 | async-start | bytes 3276800 | tf_op jit(solution)/shard_map/psum | solution.py:28
  3247.9 92.0 all-reduce.342.cloned.1.call-start
  3340.0 106.5 %all-reduce.344.cloned.1.call-start = ((), (), s32[]{:S(2)}) async-start(), calls=%async_computation.45 | async-start | bytes 3276800 | tf_op jit(solution)/shard_map/psum | solution.py:28
  3447.9 92.2 all-reduce.348.cloned.1.call-start
  3540.2 104.8 %all-reduce.350.cloned.1.call-start = ((), (), s32[]{:S(2)}) async-start(), calls=%async_computation.48 | async-start | bytes 3145728 | tf_op jit(solution)/shard_map/psum | solution.py:28
  3646.5 89.9 all-reduce.354.cloned.1.call-start
  3736.4 98.1 all-reduce.356.cloned.1.call-start
  3836.1 89.9 all-reduce.360.cloned.1.call-start
  3926.0 96.5 all-reduce.362.cloned.1.call-start
  4024.0 88.3 all-reduce.366.cloned.1.call-start
  4112.3 96.4 all-reduce.368.cloned.1.call-start
  4210.2 88.5 all-reduce.372.cloned.1.call-start
  4298.7 95.1 all-reduce.374.cloned.1.call-start
  4395.3 86.7 all-reduce.378.cloned.1.call-start
  4482.0 89.9 all-reduce.380.cloned.1.call-start
  4573.4 86.8 all-reduce.384.cloned.1.call-start
  4660.2 88.6 all-reduce.386.cloned.1.call-start
  4750.3 85.4 all-reduce.390.cloned.1.call-start
  4922.3 85.4 all-reduce.396.cloned.1.call-start
  5176.6 86.9 all-reduce.404.cloned.1.call-start
  (337 other events, 13007.3 us)
Sparse Core Ops, SparseCore 0:
  53.9 59.9 all-reduce.253
  161.9 58.2 all-reduce.257
  297.8 58.2 all-reduce.259
  403.9 58.2 all-reduce.263
  539.9 56.8 all-reduce.265
  645.3 56.8 all-reduce.269
  776.4 56.8 all-reduce.271
  881.6 56.8 all-reduce.275
  1012.8 55.4 all-reduce.277
  1116.4 55.4 all-reduce.281
  1243.4 55.4 all-reduce.283
  1347.1 55.4 all-reduce.287
  1474.2 53.9 all-reduce.289
  1576.6 54.0 all-reduce.293
  1703.3 53.9 all-reduce.295
  1805.6 54.0 all-reduce.299
  1932.4 52.5 all-reduce.301
  2032.9 52.5 all-reduce.305
  2151.6 52.5 all-reduce.307
  2252.0 52.5 all-reduce.311
  2371.1 51.0 all-reduce.313
  2469.7 51.1 all-reduce.317
  2581.2 51.1 all-reduce.319
  2679.5 51.1 all-reduce.323
  2790.9 49.7 all-reduce.325
  2886.0 49.7 all-reduce.329
  2994.6 49.7 all-reduce.331
  3089.5 49.7 all-reduce.335
  3198.1 48.2 all-reduce.337
  3291.6 48.3 all-reduce.341
  3398.1 48.2 all-reduce.343
  3491.8 48.3 all-reduce.347
  3598.1 46.8 all-reduce.349
  3689.5 46.8 all-reduce.353
  3787.7 46.8 all-reduce.355
  3879.0 46.8 all-reduce.359
  3977.0 45.4 all-reduce.361
  4066.7 45.4 all-reduce.365
  4163.2 45.4 all-reduce.367
  4253.2 45.4 all-reduce.371
  4349.8 43.9 all-reduce.373
  4437.9 44.0 all-reduce.377
  4527.9 43.9 all-reduce.379
  4616.1 44.0 all-reduce.383
  4706.2 42.5 all-reduce.385
  4793.1 42.5 all-reduce.389
  4878.2 42.5 all-reduce.391
  4965.1 42.5 all-reduce.395
  (193 shorter events, 3390.2 us)
where the time goes:
time: 9890 us; the launch traced here: 9870 us
  waiting for transfers between devices  5870 us (59%)
  other arithmetic  1830 us (19%)
  matrix products  1690 us (17%)
  local copies, waits for them, and re-layouts  399 us (4%)
    psum x63, waiting for transfers between devices, local_factor(): panel_row = lax.psum(jnp.where(is_owner, panel_blk, 0.0), 'col')  2290 us
    psum x64, waiting for transfers between devices, local_factor(): col_sum = lax.psum(work_mat[first_row:, first_col], 'rep')  2290 us
    dot_general x63, matrix products, local_factor(): jnp.einsum('tak,uck->tuac', row_share, col_share, precision=lax.Precision...  1540 us
    another operation x192, other arithmetic, local_factor(): diag_fac = jnp.tril(jnp.linalg.cholesky(lax.psum(diag_mine, 'row')))  795 us
    psum x64, waiting for transfers between devices, local_factor(): diag_fac = jnp.tril(jnp.linalg.cholesky(lax.psum(diag_mine, 'row')))  787 us
    another operation x128, other arithmetic, local_factor(): lax.linalg.triangular_solve(diag_fac, col_sum.reshape(tail_rows * blk_siz...  670 us
    all_gather x50, waiting for transfers between devices, local_factor(): gathered = lax.all_gather(panel_row, 'row', axis=1)  493 us
  transfers between devices with their start and end apart: 241, of which 241 were waited for; matrix products, arithmetic and copies ran while one was open for 1% of the time, Pallas kernels for 0%

commit v1 on v0

v1 whole, which is shorter than its diff:
```python
import jax
import jax.numpy as jnp
from jax import lax
from jax.experimental import pallas as pl
from jax.experimental.pallas import tpu as pltpu
from jax.sharding import PartitionSpec as P

MESH = pl.DeviceIdType.MESH
F32 = jnp.float32
BF16 = jnp.bfloat16
NBLK = 64
NB = 128
NSLOT = 4
NA = 6


def bc(x):
    return jnp.broadcast_to(x, (8, 128))

def cholinv(r_ref, z_ref, lt_ref):
    G = 16
    rowi = lax.broadcasted_iota(jnp.int32, (8, 128), 0)
    lanei = lax.broadcasted_iota(jnp.int32, (8, 128), 1)
    for g in range(G):
        z_ref[8*g:8*g+8, :] = jnp.where(lanei == rowi + 8*g, 1.0, 0.0).astype(jnp.float32)
    for g in range(G):
        rg = r_ref[8*g:8*g+8, :]
        zg = z_ref[8*g:8*g+8, :]
        c = [bc(rg[:, 8*g+j:8*g+j+1]) for j in range(8)]
        m = [[bc(c[b][a:a+1, :]) for b in range(a+1)] for a in range(8)]
        rr = [None]*8
        l = [[None]*8 for _ in range(8)]
        x = [[None]*8 for _ in range(8)]
        for j in range(8):
            rr[j] = lax.rsqrt(m[j][j])
            for a in range(j+1, 8):
                l[a][j] = m[a][j]*rr[j]
            for a in range(j+1, 8):
                for b in range(j+1, a+1):
                    m[a][b] = m[a][b] - l[a][j]*l[b][j]
            x[j][j] = rr[j]
            for b in range(j):
                s = l[j][b]*x[b][b]
                for cc in range(b+1, j):
                    s = s + l[j][cc]*x[cc][b]
                x[j][b] = -(rr[j]*s)
        rb = [bc(rg[j:j+1, :]) for j in range(8)]
        zb = [bc(zg[j:j+1, :]) for j in range(8)]
        def app(vb):
            y = []
            for i in range(8):
                s = x[i][0]*vb[0]
                for j in range(1, i+1):
                    s = s + x[i][j]*vb[j]
                y.append(s)
            w = []
            for j in range(8):
                s = x[j][j]*y[j]
                for i in range(j+1, 8):
                    s = s + x[i][j]*y[i]
                w.append(s)
            return y, w
        y, w = app(rb)
        yz, wz = app(zb)
        yp, zp = y[0], yz[0]
        for i in range(1, 8):
            yp = jnp.where(rowi == i, y[i], yp)
            zp = jnp.where(rowi == i, yz[i], zp)
        lt_ref[8*g:8*g+8, :] = yp
        z_ref[8*g:8*g+8, :] = zp
        for r in range(g+1, G):
            R = r_ref[8*r:8*r+8, :]
            cr = [bc(R[:, 8*g+j:8*g+j+1]) for j in range(8)]
            t = [cr[j]*w[j] for j in range(8)]
            tz = [cr[j]*wz[j] for j in range(8)]
            while len(t) > 1:
                t = [t[i]+t[i+1] for i in range(0, len(t), 2)]
                tz = [tz[i]+tz[i+1] for i in range(0, len(tz), 2)]
            r_ref[8*r:8*r+8, :] = R - t[0]
            z_ref[8*r:8*r+8, :] = z_ref[8*r:8*r+8, :] - tz[0]


def dot_nt(a, b):
    return lax.dot_general(a, b, (((1,), (1,)), ((), ())), precision=lax.Precision.HIGHEST, preferred_element_type=F32)


def dot_bf(a, b):
    return lax.dot_general(a, b, (((1,), (1,)), ((), ())), preferred_element_type=F32)


def split3(w):
    b1 = w.astype(BF16)
    r1 = w - b1.astype(F32)
    b2 = r1.astype(BF16)
    r2 = r1 - b2.astype(F32)
    return b1, b2, r2.astype(BF16)


def kernel(a_ref, out_ref, u_ref, g_ref, ac_ref, s_ref, ud_ref, ls_ref, li_ref, lkk_ref, d_ref, lt_ref, lh_ref,
           pri_send, li_recv, ls_recv, g_send, g_recv, credit, a_loc, a_send, a_recv, o_sem):
    div, rem = lax.div, lax.rem
    p, c, r = lax.axis_index("rep"), lax.axis_index("col"), lax.axis_index("row")

    def class_of(pp, cc, rr):
        return cc + 2 * (2 * pp + rem(pp + rr, 2))

    me = class_of(p, c, r)
    flips = [(0, 1, 0), (0, 1, 1), (0, 0, 1), (1, 1, 0), (1, 1, 1), (1, 0, 0), (1, 0, 1)]

    def partner(fl):
        pp = 1 - p if fl[0] else p
        cc = 1 - c if fl[1] else c
        rr = 1 - r if fl[2] else r
        return pp, cc, rr

    def dev(fl):
        pp, cc, rr = partner(fl)
        return {"rep": pp, "col": cc, "row": rr}

    SIB, XN, YN, DG = (0, 0, 1), (0, 1, 0), (1, 0, 0), (1, 1, 0)
    groups = [SIB, XN, YN, DG]

    def xor_sib(fl):
        return (fl[0], fl[1], 1 - fl[2])

    my_q = div(me, 2)
    sib_q = div(class_of(p, c, 1 - r), 2)

    def fetch_src(col, q):
        kk = div(col, 2)
        jj, qq = div(kk, 4), rem(kk, 4)
        nat = a_ref.at[:, q, jj, qq]
        tra = a_ref.at[jj, qq, :, q]
        return nat, tra

    def fetch(col):
        slot = rem(col, NA)

        @pl.when(rem(col, 2) == r)
        def _():
            nat0, tra0 = fetch_src(col, my_q)
            nat1, tra1 = fetch_src(col, sib_q)

            @pl.when(r == c)
            def _():
                pltpu.make_async_copy(nat0, ac_ref.at[slot], a_loc.at[slot]).start()
                pltpu.make_async_remote_copy(nat1, ac_ref.at[slot], a_send.at[slot], a_recv.at[slot],
                                             device_id=dev(SIB), device_id_type=MESH).start()

            @pl.when(r != c)
            def _():
                pltpu.make_async_copy(tra0, ac_ref.at[slot], a_loc.at[slot]).start()
                pltpu.make_async_remote_copy(tra1, ac_ref.at[slot], a_send.at[slot], a_recv.at[slot],
                                             device_id=dev(SIB), device_id_type=MESH).start()

    def fetch_wait(col):
        slot = rem(col, NA)
        cp = pltpu.make_async_remote_copy(ac_ref.at[slot], ac_ref.at[slot], a_send.at[slot], a_recv.at[slot],
                                          device_id=dev(SIB), device_id_type=MESH)

        @pl.when(rem(col, 2) == r)
        def _():
            pltpu.make_async_copy(ac_ref.at[slot], ac_ref.at[slot], a_loc.at[slot]).wait()
            cp.wait_send()

        @pl.when(rem(col, 2) != r)
        def _():
            cp.wait_recv()

    zb = jnp.zeros((NB, NB), F32)
    for s in range(2):
        for h in range(2):
            ls_ref[s, h] = zb
    barrier = pltpu.get_barrier_semaphore()
    for fl in flips:
        pl.semaphore_signal(barrier, inc=1, device_id=dev(fl), device_id_type=MESH)
    pl.semaphore_wait(barrier, 7)
    for col in range(3):
        fetch(jnp.int32(col))

    def zero_u(t, _):
        u_ref[t] = jnp.zeros((1024, 256), F32)
        return 0

    lax.fori_loop(0, 32, zero_u, 0)
    for i in range(8):
        ud_ref[i] = zb
        for s in (2, 3):
            g_ref[s, me, i] = zb

    def li_copy(n, k):
        slot = rem(k, 8)
        return pltpu.make_async_remote_copy(li_ref.at[slot], li_ref.at[slot], pri_send.at[0, n], li_recv.at[slot],
                                            device_id=dev(flips[n]), device_id_type=MESH)

    def ls_copy(n, k, h):
        slot = rem(k, 8)
        return pltpu.make_async_remote_copy(ls_ref.at[slot, h], ls_ref.at[slot, h], pri_send.at[1 + h, n],
                                            ls_recv.at[slot, h], device_id=dev(flips[n]), device_id_type=MESH)

    def piece_copy(t, slot, cls, ph, via):
        src = g_ref.at[slot, cls, pl.ds(ph, 8 - ph)]
        to = SIB if via else groups[t]
        idx = 3 + t if via else t
        return pltpu.make_async_remote_copy(src, src, g_send.at[slot, idx], g_recv.at[slot, idx],
                                            device_id=dev(to), device_id_type=MESH)

    def phases(k, fn):
        for ph in range(8):
            @pl.when(div(k, 8) == ph)
            def _():
                fn(ph)

    def out_copy(m, ph, e):
        kk = div(m, 2)
        return pltpu.make_async_copy(g_ref.at[rem(m, NSLOT), 2 * e + r, pl.ds(ph, 8 - ph)],
                                     out_ref.at[pl.ds(ph, 8 - ph), e, div(kk, 4), rem(kk, 4)], o_sem.at[e])

    def step(kp1, _):
        k = kp1 - 1
        nxt = kp1

        @pl.when(nxt < NBLK)
        def _():
            fetch_wait(nxt)

        active = jnp.logical_and(k >= 0, k < NBLK)
        slot_k = rem(k + 4, NSLOT)
        slot_1 = rem(k + 3, NSLOT)
        slot_2 = rem(k + 2, NSLOT)
        k0 = jnp.maximum(k, 0)
        i_first = div(k0, 8)

        @pl.when(active)
        def _():
            own_k = rem(k, 8) == me

            @pl.when(jnp.logical_and(k >= 1, jnp.logical_not(own_k)))
            def _():
                ls_copy(0, k, 1).wait_recv()

            @pl.when(jnp.logical_and(k >= 2, jnp.logical_not(own_k)))
            def _():
                ls_copy(0, k, 0).wait_recv()

            aslot = rem(k, NA)

            @pl.when(rem(k, 2) == c)
            def _():
                def cp(i, _):
                    s_ref[i] = ac_ref[aslot, i]
                    return 0
                lax.fori_loop(i_first, 8, cp, 0)

            @pl.when(rem(k, 2) != c)
            def _():
                def cp(i, _):
                    s_ref[i] = ac_ref[aslot, i].T
                    return 0
                lax.fori_loop(i_first, 8, cp, 0)

            ls0 = ls_ref[rem(k, 8), 0]
            ls1 = ls_ref[rem(k, 8), 1]
            lane0 = pl.multiple_of(rem(k, 2) * NB, NB)

            def upd(i2, _):
                rows = pl.ds(pl.multiple_of(i2 * 256, 256), 256)
                acc = dot_nt(g_ref[slot_1, me, pl.ds(2 * i2, 2)].reshape(256, NB), ls1)
                acc = acc + dot_nt(g_ref[slot_2, me, pl.ds(2 * i2, 2)].reshape(256, NB), ls0)
                acc = acc + u_ref[div(k, 2), rows, pl.ds(lane0, NB)]
                s_ref[pl.ds(2 * i2, 2)] = s_ref[pl.ds(2 * i2, 2)] - acc.reshape(2, NB, NB)
                return 0
            lax.fori_loop(div(i_first, 2), 4, upd, 0)

            @pl.when(jnp.logical_not(own_k))
            def _():
                li_copy(0, k).wait_recv()

        @pl.when(jnp.logical_and(nxt < NBLK, rem(nxt, 8) == me))
        def _():
            i_n = div(nxt, 8)
            sl = rem(nxt, 8)
            d0 = ac_ref[rem(nxt, NA), i_n] - ud_ref[i_n]

            @pl.when(k >= 0)
            def _():
                xs = dot_nt(s_ref[i_n], li_ref[rem(k0, 8)])
                ls_ref[sl, 1] = xs
                for n in range(7):
                    ls_copy(n, nxt, 1).start()
                d_ref[...] = d0 - dot_nt(xs, xs)

            @pl.when(k < 0)
            def _():
                d_ref[...] = d0

            cholinv(d_ref, li_ref.at[sl], lt_ref)
            for n in range(7):
                li_copy(n, nxt).start()
            ri = lax.broadcasted_iota(jnp.int32, (NB, NB), 0)
            ci = lax.broadcasted_iota(jnp.int32, (NB, NB), 1)
            lkk_ref[...] = jnp.where(ri >= ci, lt_ref[...].T, 0.0)

        @pl.when(active)
        def _():
            li = li_ref[rem(k, 8)]
            lkk = lkk_ref[...]

            def solve(i, _):
                x = dot_nt(s_ref[i], li)
                gi = 8 * i + me
                x = jnp.where(gi > k, x, jnp.where(gi == k, lkk, jnp.zeros_like(x)))
                g_ref[slot_k, me, i] = x
                ud_ref[i] = ud_ref[i] + dot_nt(x, x)
                b1, b2, b3 = split3(x)
                rows = pl.ds(pl.multiple_of(i * NB, NB), NB)
                lh_ref[slot_k, rows, 0:NB] = b2
                lh_ref[slot_k, rows, NB:2 * NB] = b1
                lh_ref[slot_k, rows, 2 * NB:3 * NB] = b3
                return 0
            lax.fori_loop(i_first, 8, solve, 0)

            @pl.when(jnp.logical_and(k + 2 < NBLK, rem(k + 2, 8) == me))
            def _():
                ls_ref[rem(k + 2, 8), 0] = g_ref[slot_k, me, div(k + 2, 8)]
                for n in range(7):
                    ls_copy(n, k + 2, 0).start()

            @pl.when(rem(k, 8) == me)
            def _():
                for n in range(7):
                    li_copy(n, k).wait_send()

                @pl.when(k >= 1)
                def _():
                    for n in range(7):
                        ls_copy(n, k, 1).wait_send()

                @pl.when(k >= 2)
                def _():
                    for n in range(7):
                        ls_copy(n, k, 0).wait_send()

            @pl.when(k >= NSLOT)
            def _():
                for t in range(4):
                    pl.semaphore_wait(credit.at[t], 1)

            def send(ph):
                for t in range(4):
                    piece_copy(t, slot_k, me, ph, False).start()
            phases(k, send)

        @pl.when(jnp.logical_and(k >= 1, k <= NBLK))
        def _():
            def fwd(ph):
                for t in range(1, 4):
                    cls = class_of(*partner(groups[t]))
                    piece_copy(t, slot_1, cls, ph, False).wait_recv()
                    piece_copy(t, slot_1, cls, ph, True).start()
            phases(k - 1, fwd)

        @pl.when(k >= 2)
        def _():
            m = k - 2

            def arrive(ph):
                piece_copy(0, slot_2, class_of(*partner(SIB)), ph, False).wait_recv()
                for t in range(1, 4):
                    piece_copy(t, slot_2, class_of(*partner(xor_sib(groups[t]))), ph, True).wait_recv()

                @pl.when(rem(m, 2) == c)
                def _():
                    for e in range(4):
                        out_copy(m, ph, e).start()
            phases(m, arrive)

            for v in range(4):
                def bulk(jp, _):
                    i = div(jp, 4)
                    jc = 2 * rem(jp, 4)
                    w0 = split3(g_ref[slot_2, jc, i])
                    w1 = split3(g_ref[slot_2, jc + 1, i])
                    b1, b2, b3 = [jnp.concatenate([x0, x1], axis=0) for x0, x1 in zip(w0, w1)]
                    r1 = jnp.concatenate([b1, b1], axis=1)
                    r2 = jnp.concatenate([b2, b2], axis=1)
                    r3 = jnp.concatenate([b3, b1], axis=1)
                    for ch in range(v, 4):
                        rows = pl.ds(ch * 256, 256)
                        l12 = lh_ref[slot_2, rows, 0:256]
                        l13 = lh_ref[slot_2, rows, 128:384]
                        acc = dot_bf(l12, r1) + dot_bf(l12, r2) + dot_bf(l13, r3)
                        u_ref[jp, rows, :] = u_ref[jp, rows, :] + acc
                    return 0
                lax.fori_loop(jnp.maximum(div(m + 3, 2), 8 * v), 8 * v + 8, bulk, 0)

            def finish(ph):
                for t in range(4):
                    piece_copy(t, slot_2, me, ph, False).wait_send()
                for t in range(1, 4):
                    piece_copy(t, slot_2, class_of(*partner(groups[t])), ph, True).wait_send()

                @pl.when(rem(m, 2) == c)
                def _():
                    for e in range(4):
                        out_copy(m, ph, e).wait()
            phases(m, finish)

            @pl.when(m + NSLOT < NBLK)
            def _():
                for t in range(4):
                    pl.semaphore_signal(credit.at[t], inc=1, device_id=dev(groups[t]), device_id_type=MESH)

        @pl.when(k + 4 < NBLK)
        def _():
            fetch(k + 4)
        return 0

    lax.fori_loop(0, NBLK + 3, step, 0)


def solution(mesh):
    grid_spec = P(("b", "row"), "col")

    def local_factor(a_loc):
        a6 = a_loc.reshape(8, 4, 8, 4, NB, NB)
        dma = pltpu.SemaphoreType.DMA
        fac = pl.pallas_call(
            kernel,
            out_shape=jax.ShapeDtypeStruct((8, 4, 8, 4, NB, NB), F32),
            in_specs=[pl.BlockSpec(memory_space=pl.ANY)],
            out_specs=pl.BlockSpec(memory_space=pl.ANY),
            scratch_shapes=[
                pltpu.VMEM((32, 1024, 256), F32),
                pltpu.VMEM((NSLOT, 8, 8, NB, NB), F32),
                pltpu.VMEM((NA, 8, NB, NB), F32),
                pltpu.VMEM((8, NB, NB), F32),
                pltpu.VMEM((8, NB, NB), F32),
                pltpu.VMEM((8, 2, NB, NB), F32),
                pltpu.VMEM((8, NB, NB), F32),
                pltpu.VMEM((NB, NB), F32),
                pltpu.VMEM((NB, NB), F32),
                pltpu.VMEM((NB, NB), F32),
                pltpu.VMEM((NSLOT, 1024, 384), BF16),
                dma((3, 7)),
                dma((8,)),
                dma((8, 2)),
                dma((NSLOT, 7)),
                dma((NSLOT, 7)),
                pltpu.SemaphoreType.REGULAR((4,)),
                dma((NA,)),
                dma((NA,)),
                dma((NA,)),
                dma((4,)),
            ],
            compiler_params=pltpu.CompilerParams(
                collective_id=0, has_side_effects=True, vmem_limit_bytes=67043328),
            name="chol_all",
        )(a6)
        fac = fac.reshape(32, 32, NB, NB)
        gi = 2 * jnp.arange(32) + lax.axis_index("row")
        gj = 2 * jnp.arange(32) + lax.axis_index("col")
        keep = gi[:, None] >= gj[None, :]
        return jnp.where(keep[:, :, None, None], fac, 0.0)

    return jax.shard_map(local_factor, mesh=mesh, in_specs=grid_spec, out_specs=grid_spec, check_vma=False)
```

time: 9890 us -> 1120 us (0.11)
  waiting for transfers between devices: 5870 us -> 0 us
  other arithmetic: 1830 us -> 45.2 us
  matrix products: 1690 us -> 0 us
  Pallas kernels: 0 us -> 1080 us
  local copies, waits for them, and re-layouts: 399 us -> 0 us
    psum x191 -> x0, waiting for transfers between devices: 5370 us -> none  [the longest x63 2290 us: local_factor(): panel_row = lax.psum(jnp.where(is_owner, panel_blk, 0.0), 'col')]
    dot_general x63 -> x0, matrix products: 1540 us -> none  [local_factor(): jnp.einsum('tak,uck->tuac', row_share, col_share, precision=lax.Precision...]
    another operation x321 -> x0, other arithmetic: 1470 us -> none  [the longest x192 795 us: local_factor(): diag_fac = jnp.tril(jnp.linalg.cholesky(lax.psum(diag_mine, 'row')))]
    pallas_call x0 -> x1, Pallas kernels: none -> 1080 us  [local_factor(): pl.pallas_call(kernel, out_shape=jax.ShapeDtypeStruct((8, 4, 8, 4, NB, NB...]
    all_gather x50 -> x0, waiting for transfers between devices: 493 us -> none  [local_factor(): gathered = lax.all_gather(panel_row, 'row', axis=1)]
    select_n x128 -> x1, other arithmetic: 250 us -> 44.6 us  [local_factor(): return jnp.where(keep[:, :, None, None], fac, 0.0)]
    another operation x64 -> x0, matrix products: 150 us -> none  [local_factor(): lax.linalg.triangular_solve(diag_fac, col_sum.reshape(tail_rows * blk_siz...]
    unnamed x288 -> x0, local copies, waits for them, and re-layouts: 145 us -> none
  transfers between devices with their start and end apart: 241 -> 0, of which waited for: 241 -> 0; matrix products, arithmetic and copies ran while one was open for 1% -> 0% of each run, Pallas kernels for 0% -> 0%
where the time goes in v1:
time: 1120 us
  Pallas kernels  1080 us (96%)
  other arithmetic  45.2 us (4%)
    pallas_call x1, Pallas kernels, local_factor(): pl.pallas_call(kernel, out_shape=jax.ShapeDtypeStruct((8, 4, 8, 4, NB, NB...  1080 us
    select_n x1, other arithmetic, local_factor(): return jnp.where(keep[:, :, None, None], fac, 0.0)  44.6 us

profile of v1, /device:TPU:0, one launch (start us, length us, event | category | flops | bytes accessed | tf_op | source)
XLA Modules:
  0.0 1122.1 jit_solution(9305092134029910077)
XLA Ops:
  0.0 0.7 broadcast_compare_fusion
  0.7 1076.8 %chol_all.1 = f32[8,4,8,4,128,128]{5,4,3,2,1,0:T(8,128)} custom-call(f32[8,4,8,4,128,128]{5,4,3,2,1,0:T(8,128)} %bitcast.a_ref), custom_call_target="tpu_custom_call" | custom-call | tf_op jit(solution)/shard_map/chol_all/pallas_call | solution.py:428
  1077.5 44.6 %broadcast_select_fusion = f32[32,32,128,128]{3,2,1,0:T(8,128)} fusion(f32[32,32,128,128]{3,2,1,0:T(8,128)} %bitcast.1, pred[32,32]{1,0:T(8,128)(4,1)} %broadcast_compare_fusion), kind=kLoop, calls=%fused_computation | loop fusion | flops 16777216 | bytes 134218752 | tf_op jit(solution)/shard_map/jit(_where)/select_n | solution.py:464
  (1 shorter events, 0.0 us)

commit v2 on v1

--- a/solution.py
+++ b/solution.py
@@ -96,7 +96,19 @@
     return b1, b2, r2.astype(BF16)
 
 
-def kernel(a_ref, out_ref, u_ref, g_ref, ac_ref, s_ref, ud_ref, ls_ref, li_ref, lkk_ref, d_ref, lt_ref, lh_ref,
+def dot6(lhs, rhs):
+    b1, b2, b3 = rhs
+    acc = dot_bf(lhs[:, 0:256], jnp.concatenate([b1, b1], axis=1))
+    acc = acc + dot_bf(lhs[:, 0:256], jnp.concatenate([b2, b2], axis=1))
+    return acc + dot_bf(lhs[:, 128:384], jnp.concatenate([b3, b1], axis=1))
+
+
+def parts_lhs(x):
+    b1, b2, b3 = split3(x)
+    return jnp.concatenate([b2, b1, b3], axis=1)
+
+
+def kernel(a_ref, out_ref, u_ref, g_ref, ac_ref, s_ref, ls_ref, li_ref, lkk_ref, d_ref, lt_ref, lh_ref,
            pri_send, li_recv, ls_recv, g_send, g_recv, credit, a_loc, a_send, a_recv, o_sem):
     div, rem = lax.div, lax.rem
     p, c, r = lax.axis_index("rep"), lax.axis_index("col"), lax.axis_index("row")
@@ -183,20 +195,35 @@
         return 0
 
     lax.fori_loop(0, 32, zero_u, 0)
-    for i in range(8):
-        ud_ref[i] = zb
-        for s in (2, 3):
+    for s in (2, 3):
+        lh_ref[s] = jnp.zeros((1024, 384), BF16)
+        for i in range(8):
             g_ref[s, me, i] = zb
+
+    def pri_dev(n, k):
+        if n == 3:
+            return dev(SIB)
+        pp, cc, _ = partner([XN, DG, YN][n])
+        rr = jnp.where(rem(k, 4) == 1, 1 - r, r)
+        return {"rep": pp, "col": cc, "row": rr}
 
     def li_copy(n, k):
         slot = rem(k, 8)
         return pltpu.make_async_remote_copy(li_ref.at[slot], li_ref.at[slot], pri_send.at[0, n], li_recv.at[slot],
-                                            device_id=dev(flips[n]), device_id_type=MESH)
+                                            device_id=pri_dev(n, k), device_id_type=MESH)
 
     def ls_copy(n, k, h):
         slot = rem(k, 8)
         return pltpu.make_async_remote_copy(ls_ref.at[slot, h], ls_ref.at[slot, h], pri_send.at[1 + h, n],
-                                            ls_recv.at[slot, h], device_id=dev(flips[n]), device_id_type=MESH)
+                                            ls_recv.at[slot, h], device_id=pri_dev(n, k), device_id_type=MESH)
+
+    def hands_on(k):
+        q_o = rem(div(k, 2), 4)
+        p_o = div(q_o, 2)
+        r_o = rem(q_o + p_o, 2)
+        turn = jnp.where(rem(k, 4) == 1, 1, 0)
+        away = jnp.logical_or(p != p_o, c != rem(k, 2))
+        return jnp.logical_and(away, r == rem(r_o + turn, 2))
 
     def piece_copy(t, slot, cls, ph, via):
         src = g_ref.at[slot, cls, pl.ds(ph, 8 - ph)]
@@ -205,9 +232,17 @@
         return pltpu.make_async_remote_copy(src, src, g_send.at[slot, idx], g_recv.at[slot, idx],
                                             device_id=dev(to), device_id_type=MESH)
 
-    def phases(k, fn):
+    def relay_copy(slot, cls, ph, to):
+        src = g_ref.at[slot, cls, pl.ds(ph, 8 - ph)]
+        return pltpu.make_async_remote_copy(src, src, g_send.at[slot, 3], g_recv.at[slot, 3],
+                                            device_id=dev(to), device_id_type=MESH)
+
+    def first_of(k, cls):
+        return div(k - cls + 7, 8)
+
+    def phases(k, cls, fn):
         for ph in range(8):
-            @pl.when(div(k, 8) == ph)
+            @pl.when(first_of(k, cls) == ph)
             def _():
                 fn(ph)
 
@@ -229,73 +264,81 @@
         slot_1 = rem(k + 3, NSLOT)
         slot_2 = rem(k + 2, NSLOT)
         k0 = jnp.maximum(k, 0)
-        i_first = div(k0, 8)
 
         @pl.when(active)
         def _():
             own_k = rem(k, 8) == me
 
-            @pl.when(jnp.logical_and(k >= 1, jnp.logical_not(own_k)))
-            def _():
-                ls_copy(0, k, 1).wait_recv()
-
-            @pl.when(jnp.logical_and(k >= 2, jnp.logical_not(own_k)))
-            def _():
-                ls_copy(0, k, 0).wait_recv()
+            hand = hands_on(k)
+            for h in (0, 1):
+                @pl.when(jnp.logical_and(k >= 2 - h, jnp.logical_not(own_k)))
+                def _():
+                    ls_copy(3, k, h).wait_recv()
+
+                    @pl.when(hand)
+                    def _():
+                        ls_copy(3, k, h).start()
 
             aslot = rem(k, NA)
-
-            @pl.when(rem(k, 2) == c)
-            def _():
-                def cp(i, _):
-                    s_ref[i] = ac_ref[aslot, i]
-                    return 0
-                lax.fori_loop(i_first, 8, cp, 0)
-
-            @pl.when(rem(k, 2) != c)
-            def _():
-                def cp(i, _):
-                    s_ref[i] = ac_ref[aslot, i].T
-                    return 0
-                lax.fori_loop(i_first, 8, cp, 0)
-
-            ls0 = ls_ref[rem(k, 8), 0]
-            ls1 = ls_ref[rem(k, 8), 1]
+            ls0 = split3(ls_ref[rem(k, 8), 0])
+            ls1 = split3(ls_ref[rem(k, 8), 1])
             lane0 = pl.multiple_of(rem(k, 2) * NB, NB)
 
-            def upd(i2, _):
-                rows = pl.ds(pl.multiple_of(i2 * 256, 256), 256)
-                acc = dot_nt(g_ref[slot_1, me, pl.ds(2 * i2, 2)].reshape(256, NB), ls1)
-                acc = acc + dot_nt(g_ref[slot_2, me, pl.ds(2 * i2, 2)].reshape(256, NB), ls0)
-                acc = acc + u_ref[div(k, 2), rows, pl.ds(lane0, NB)]
-                s_ref[pl.ds(2 * i2, 2)] = s_ref[pl.ds(2 * i2, 2)] - acc.reshape(2, NB, NB)
-                return 0
-            lax.fori_loop(div(i_first, 2), 4, upd, 0)
+            def update(ph):
+                n = 1024 - NB * ph
+                rows = pl.ds(NB * ph, n)
+
+                @pl.when(rem(k, 2) == c)
+                def _():
+                    s_ref[rows, :] = ac_ref[aslot, ph:8].reshape(n, NB)
+
+                @pl.when(rem(k, 2) != c)
+                def _():
+                    for i in range(ph, 8):
+                        s_ref[i * NB:(i + 1) * NB, :] = ac_ref[aslot, i].T
+
+                acc = dot6(lh_ref[slot_1, rows, :], ls1) + dot6(lh_ref[slot_2, rows, :], ls0)
+                s_ref[rows, :] = s_ref[rows, :] - (u_ref[div(k, 2), rows, pl.ds(lane0, NB)] + acc)
+            phases(k, me, update)
+
+            @pl.when(jnp.logical_and(nxt < NBLK, rem(nxt, 8) == me))
+            def _():
+                i_n = div(nxt, 8)
+                lane_n = pl.multiple_of(rem(nxt, 2) * NB, NB)
+                rows_n = pl.ds(pl.multiple_of(i_n * NB, NB), NB)
+                p1 = g_ref[slot_1, me, i_n]
+                p2 = g_ref[slot_2, me, i_n]
+                d_ref[...] = (ac_ref[rem(nxt, NA), i_n] - u_ref[div(nxt, 2), rows_n, pl.ds(lane_n, NB)]
+                              - (dot_nt(p1, p1) + dot_nt(p2, p2)))
 
             @pl.when(jnp.logical_not(own_k))
             def _():
-                li_copy(0, k).wait_recv()
+                li_copy(3, k).wait_recv()
+
+                @pl.when(hand)
+                def _():
+                    li_copy(3, k).start()
 
         @pl.when(jnp.logical_and(nxt < NBLK, rem(nxt, 8) == me))
         def _():
             i_n = div(nxt, 8)
             sl = rem(nxt, 8)
-            d0 = ac_ref[rem(nxt, NA), i_n] - ud_ref[i_n]
+            rows_n = pl.ds(pl.multiple_of(i_n * NB, NB), NB)
+
+            @pl.when(k < 0)
+            def _():
+                d_ref[...] = ac_ref[0, 0]
 
             @pl.when(k >= 0)
             def _():
-                xs = dot_nt(s_ref[i_n], li_ref[rem(k0, 8)])
+                xs = dot_nt(s_ref[rows_n, :], li_ref[rem(k0, 8)])
                 ls_ref[sl, 1] = xs
-                for n in range(7):
+                for n in range(4):
                     ls_copy(n, nxt, 1).start()
-                d_ref[...] = d0 - dot_nt(xs, xs)
-
-            @pl.when(k < 0)
-            def _():
-                d_ref[...] = d0
+                d_ref[...] = d_ref[...] - dot_nt(xs, xs)
 
             cholinv(d_ref, li_ref.at[sl], lt_ref)
-            for n in range(7):
+            for n in range(4):
                 li_copy(n, nxt).start()
             ri = lax.broadcasted_iota(jnp.int32, (NB, NB), 0)
             ci = lax.broadcasted_iota(jnp.int32, (NB, NB), 1)
@@ -306,109 +349,130 @@
             li = li_ref[rem(k, 8)]
             lkk = lkk_ref[...]
 
-            def solve(i, _):
-                x = dot_nt(s_ref[i], li)
-                gi = 8 * i + me
-                x = jnp.where(gi > k, x, jnp.where(gi == k, lkk, jnp.zeros_like(x)))
-                g_ref[slot_k, me, i] = x
-                ud_ref[i] = ud_ref[i] + dot_nt(x, x)
-                b1, b2, b3 = split3(x)
-                rows = pl.ds(pl.multiple_of(i * NB, NB), NB)
-                lh_ref[slot_k, rows, 0:NB] = b2
-                lh_ref[slot_k, rows, NB:2 * NB] = b1
-                lh_ref[slot_k, rows, 2 * NB:3 * NB] = b3
-                return 0
-            lax.fori_loop(i_first, 8, solve, 0)
+            li3 = split3(li)
+
+            def solve(ph):
+                n = 1024 - NB * ph
+                rows = pl.ds(NB * ph, n)
+                x = dot6(parts_lhs(s_ref[rows, :]), li3)
+                g_ref[slot_k, me, ph:8] = x.reshape(8 - ph, NB, NB)
+                lh_ref[slot_k, rows, :] = parts_lhs(x)
+
+                @pl.when(8 * ph + me == k)
+                def _():
+                    g_ref[slot_k, me, ph] = lkk
+            phases(k, me, solve)
 
             @pl.when(jnp.logical_and(k + 2 < NBLK, rem(k + 2, 8) == me))
             def _():
                 ls_ref[rem(k + 2, 8), 0] = g_ref[slot_k, me, div(k + 2, 8)]
-                for n in range(7):
+                for n in range(4):
                     ls_copy(n, k + 2, 0).start()
 
-            @pl.when(rem(k, 8) == me)
-            def _():
-                for n in range(7):
+            for n in range(4):
+                sent = rem(k, 8) == me
+                if n == 3:
+                    sent = jnp.logical_or(sent, hands_on(k))
+
+                @pl.when(sent)
+                def _():
                     li_copy(n, k).wait_send()
-
-                @pl.when(k >= 1)
-                def _():
-                    for n in range(7):
-                        ls_copy(n, k, 1).wait_send()
-
-                @pl.when(k >= 2)
-                def _():
-                    for n in range(7):
-                        ls_copy(n, k, 0).wait_send()
+                for h in (0, 1):
+                    @pl.when(jnp.logical_and(sent, k >= 2 - h))
+                    def _():
+                        ls_copy(n, k, h).wait_send()
 
             @pl.when(k >= NSLOT)
             def _():
-                for t in range(4):
+                for t in range(3):
                     pl.semaphore_wait(credit.at[t], 1)
 
             def send(ph):
-                for t in range(4):
+                for t in range(3):
                     piece_copy(t, slot_k, me, ph, False).start()
-            phases(k, send)
+            phases(k, me, send)
 
         @pl.when(jnp.logical_and(k >= 1, k <= NBLK))
         def _():
-            def fwd(ph):
-                for t in range(1, 4):
-                    cls = class_of(*partner(groups[t]))
+            for t, to, odd in ((1, YN, 0), (2, XN, 1)):
+                cls = class_of(*partner(groups[t]))
+
+                def fwd(ph):
                     piece_copy(t, slot_1, cls, ph, False).wait_recv()
                     piece_copy(t, slot_1, cls, ph, True).start()
-            phases(k - 1, fwd)
+
+                    @pl.when(rem(k - 1, 2) == odd)
+                    def _():
+                        relay_copy(slot_1, cls, ph, to).start()
+                phases(k - 1, cls, fwd)
 
         @pl.when(k >= 2)
         def _():
             m = k - 2
-
-            def arrive(ph):
-                piece_copy(0, slot_2, class_of(*partner(SIB)), ph, False).wait_recv()
-                for t in range(1, 4):
-                    piece_copy(t, slot_2, class_of(*partner(xor_sib(groups[t]))), ph, True).wait_recv()
-
-                @pl.when(rem(m, 2) == c)
-                def _():
-                    for e in range(4):
-                        out_copy(m, ph, e).start()
-            phases(m, arrive)
-
-            for v in range(4):
-                def bulk(jp, _):
-                    i = div(jp, 4)
+            dg_cls = class_of(*partner(DG))
+
+            def fwd_dg(ph):
+                piece_copy(3, slot_2, dg_cls, ph, False).wait_recv()
+                piece_copy(3, slot_2, dg_cls, ph, True).start()
+            phases(m, dg_cls, fwd_dg)
+
+            sib_cls = class_of(*partner(SIB))
+            phases(m, sib_cls, lambda ph: piece_copy(0, slot_2, sib_cls, ph, False).wait_recv())
+            for t in range(1, 4):
+                cls = class_of(*partner(xor_sib(groups[t])))
+                phases(m, cls, lambda ph: piece_copy(t, slot_2, cls, ph, True).wait_recv())
+
+            @pl.when(rem(m, 2) == c)
+            def _():
+                for e in range(4):
+                    phases(m, 2 * e + r, lambda ph: out_copy(m, ph, e).start())
+
+            start = div(m + 3, 2)
+            for v in range(8):
+                rows = pl.ds(NB * v, 1024 - NB * v)
+
+                def bulk(jp, v=v, rows=rows):
                     jc = 2 * rem(jp, 4)
-                    w0 = split3(g_ref[slot_2, jc, i])
-                    w1 = split3(g_ref[slot_2, jc + 1, i])
-                    b1, b2, b3 = [jnp.concatenate([x0, x1], axis=0) for x0, x1 in zip(w0, w1)]
-                    r1 = jnp.concatenate([b1, b1], axis=1)
-                    r2 = jnp.concatenate([b2, b2], axis=1)
-                    r3 = jnp.concatenate([b3, b1], axis=1)
-                    for ch in range(v, 4):
-                        rows = pl.ds(ch * 256, 256)
-                        l12 = lh_ref[slot_2, rows, 0:256]
-                        l13 = lh_ref[slot_2, rows, 128:384]
-                        acc = dot_bf(l12, r1) + dot_bf(l12, r2) + dot_bf(l13, r3)
-                        u_ref[jp, rows, :] = u_ref[jp, rows, :] + acc
-                    return 0
-                lax.fori_loop(jnp.maximum(div(m + 3, 2), 8 * v), 8 * v + 8, bulk, 0)
+                    w0 = split3(g_ref[slot_2, jc, v])
+                    w1 = split3(g_ref[slot_2, jc + 1, v])
+                    w = [jnp.concatenate([x0, x1], axis=0) for x0, x1 in zip(w0, w1)]
+                    u_ref[jp, rows, :] = u_ref[jp, rows, :] + dot6(lh_ref[slot_2, rows, :], w)
+
+                @pl.when(start <= 4 * v)
+                def _():
+                    for q in range(4):
+                        bulk(4 * v + q)
+
+                @pl.when(jnp.logical_and(start > 4 * v, start < 4 * v + 4))
+                def _():
+                    def one(jp, _):
+                        bulk(jp)
+                        return 0
+                    lax.fori_loop(start, 4 * v + 4, one, 0)
 
             def finish(ph):
-                for t in range(4):
+                for t in range(3):
                     piece_copy(t, slot_2, me, ph, False).wait_send()
-                for t in range(1, 4):
-                    piece_copy(t, slot_2, class_of(*partner(groups[t])), ph, True).wait_send()
-
-                @pl.when(rem(m, 2) == c)
-                def _():
-                    for e in range(4):
-                        out_copy(m, ph, e).wait()
-            phases(m, finish)
+            phases(m, me, finish)
+            for t in range(1, 4):
+                cls = class_of(*partner(groups[t]))
+
+                def finish_fwd(ph):
+                    piece_copy(t, slot_2, cls, ph, True).wait_send()
+                    if t < 3:
+                        @pl.when(rem(m, 2) == t - 1)
+                        def _():
+                            relay_copy(slot_2, cls, ph, YN).wait_send()
+                phases(m, cls, finish_fwd)
+
+            @pl.when(rem(m, 2) == c)
+            def _():
+                for e in range(4):
+                    phases(m, 2 * e + r, lambda ph: out_copy(m, ph, e).wait())
 
             @pl.when(m + NSLOT < NBLK)
             def _():
-                for t in range(4):
+                for t in range(3):
                     pl.semaphore_signal(credit.at[t], inc=1, device_id=dev(groups[t]), device_id_type=MESH)
 
         @pl.when(k + 4 < NBLK)
@@ -434,20 +498,19 @@
                 pltpu.VMEM((32, 1024, 256), F32),
                 pltpu.VMEM((NSLOT, 8, 8, NB, NB), F32),
                 pltpu.VMEM((NA, 8, NB, NB), F32),
-                pltpu.VMEM((8, NB, NB), F32),
-                pltpu.VMEM((8, NB, NB), F32),
+                pltpu.VMEM((1024, NB), F32),
                 pltpu.VMEM((8, 2, NB, NB), F32),
                 pltpu.VMEM((8, NB, NB), F32),
                 pltpu.VMEM((NB, NB), F32),
                 pltpu.VMEM((NB, NB), F32),
                 pltpu.VMEM((NB, NB), F32),
                 pltpu.VMEM((NSLOT, 1024, 384), BF16),
-                dma((3, 7)),
+                dma((3, 4)),
                 dma((8,)),
                 dma((8, 2)),
                 dma((NSLOT, 7)),
                 dma((NSLOT, 7)),
-                pltpu.SemaphoreType.REGULAR((4,)),
+                pltpu.SemaphoreType.REGULAR((3,)),
                 dma((NA,)),
                 dma((NA,)),
                 dma((NA,)),

time: 1120 us -> 859 us (0.77)
  Pallas kernels: 1080 us -> 814 us
    pallas_call x1, Pallas kernels: 1080 us -> 814 us  [local_factor(): pl.pallas_call(kernel, out_shape=jax.ShapeDtypeStruct((8, 4, 8, 4, NB, NB...]
where the time goes in v2:
time: 859 us
  Pallas kernels  814 us (95%)
  other arithmetic  45.2 us (5%)
    pallas_call x1, Pallas kernels, local_factor(): pl.pallas_call(kernel, out_shape=jax.ShapeDtypeStruct((8, 4, 8, 4, NB, NB...  814 us
    select_n x1, other arithmetic, local_factor(): return jnp.where(keep[:, :, None, None], fac, 0.0)  44.6 us

profile of v2, /device:TPU:0, one launch (start us, length us, event | category | flops | bytes accessed | tf_op | source)
XLA Modules:
  0.0 858.8 jit_solution(2441926780944066034)
XLA Ops:
  0.0 0.7 broadcast_compare_fusion
  0.7 813.6 %chol_all.1 = f32[8,4,8,4,128,128]{5,4,3,2,1,0:T(8,128)} custom-call(f32[8,4,8,4,128,128]{5,4,3,2,1,0:T(8,128)} %bitcast.a_ref), custom_call_target="tpu_custom_call" | custom-call | tf_op jit(solution)/shard_map/chol_all/pallas_call | solution.py:492
  814.3 44.6 %broadcast_select_fusion = f32[32,32,128,128]{3,2,1,0:T(8,128)} fusion(f32[32,32,128,128]{3,2,1,0:T(8,128)} %bitcast.1, pred[32,32]{1,0:T(8,128)(4,1)} %broadcast_compare_fusion), kind=kLoop, calls=%fused_computation | loop fusion | flops 16777216 | bytes 134218752 | tf_op jit(solution)/shard_map/jit(_where)/select_n | solution.py:527
  (1 shorter events, 0.0 us)

commit v3 on v2

--- a/solution.py
+++ b/solution.py
@@ -12,6 +12,7 @@
 NB = 128
 NSLOT = 4
 NA = 6
+NP = 16
 
 
 def bc(x):
@@ -46,13 +47,14 @@
                 x[j][b] = -(rr[j]*s)
         rb = [bc(rg[j:j+1, :]) for j in range(8)]
         zb = [bc(zg[j:j+1, :]) for j in range(8)]
+
         def app(vb):
             y = []
             for i in range(8):
-                s = x[i][0]*vb[0]
-                for j in range(1, i+1):
-                    s = s + x[i][j]*vb[j]
-                y.append(s)
+                s = vb[i]
+                for j in range(i):
+                    s = s - l[i][j]*y[j]
+                y.append(s*rr[i])
             w = []
             for j in range(8):
                 s = x[j][j]*y[j]
@@ -109,7 +111,8 @@
 
 
 def kernel(a_ref, out_ref, u_ref, g_ref, ac_ref, s_ref, ls_ref, li_ref, lkk_ref, d_ref, lt_ref, lh_ref,
-           pri_send, li_recv, ls_recv, g_send, g_recv, credit, a_loc, a_send, a_recv, o_sem):
+           pri_send, li_recv, ls_recv, g_send, g_recv, credit, a_loc, a_send, a_recv, o_sem,
+           o3_sem, lk_send, lk_recv, a_free):
     div, rem = lax.div, lax.rem
     p, c, r = lax.axis_index("rep"), lax.axis_index("col"), lax.axis_index("row")
 
@@ -208,14 +211,40 @@
         return {"rep": pp, "col": cc, "row": rr}
 
     def li_copy(n, k):
-        slot = rem(k, 8)
+        slot = rem(k, NP)
         return pltpu.make_async_remote_copy(li_ref.at[slot], li_ref.at[slot], pri_send.at[0, n], li_recv.at[slot],
                                             device_id=pri_dev(n, k), device_id_type=MESH)
 
     def ls_copy(n, k, h):
-        slot = rem(k, 8)
+        slot = rem(k, NP)
         return pltpu.make_async_remote_copy(ls_ref.at[slot, h], ls_ref.at[slot, h], pri_send.at[1 + h, n],
                                             ls_recv.at[slot, h], device_id=pri_dev(n, k), device_id_type=MESH)
+
+    def lk_copy(n, k):
+        slot = rem(k, NP)
+        to = {"rep": p if n == 0 else 1 - p, "col": c, "row": c}
+        return pltpu.make_async_remote_copy(lkk_ref.at[slot], lkk_ref.at[slot], lk_send.at[n], lk_recv.at[slot],
+                                            device_id=to, device_id_type=MESH)
+
+    def row_copy(n, k):
+        src = [ls_ref.at[rem(k, NP), 0], ls_ref.at[rem(k, NP), 1], lkk_ref.at[rem(k, NP)]][n]
+        kk = div(k - [2, 1, 0][n], 2)
+        return pltpu.make_async_copy(src, out_ref.at[div(k, 8), div(rem(k, 8), 2), div(kk, 4), rem(kk, 4)], o3_sem.at[n])
+
+    def row_outs(k, fn):
+        @pl.when(jnp.logical_and(rem(k, 2) == r, c != r))
+        def _():
+            @pl.when(k >= 1)
+            def _():
+                fn(1)
+
+        @pl.when(jnp.logical_and(rem(k, 2) == r, c == r))
+        def _():
+            fn(2)
+
+            @pl.when(k >= 2)
+            def _():
+                fn(0)
 
     def hands_on(k):
         q_o = rem(div(k, 2), 4)
@@ -232,10 +261,24 @@
         return pltpu.make_async_remote_copy(src, src, g_send.at[slot, idx], g_recv.at[slot, idx],
                                             device_id=dev(to), device_id_type=MESH)
 
-    def relay_copy(slot, cls, ph, to):
-        src = g_ref.at[slot, cls, pl.ds(ph, 8 - ph)]
-        return pltpu.make_async_remote_copy(src, src, g_send.at[slot, 3], g_recv.at[slot, 3],
-                                            device_id=dev(to), device_id_type=MESH)
+    def relay_copy(slot, cls, ph, h, t):
+        lo, hi = (ph, ph + h) if t == 1 else (ph + h, 8)
+        src = g_ref.at[slot, cls, pl.ds(lo, hi - lo)]
+        idx = 3 if t == 1 else 7
+        return pltpu.make_async_remote_copy(src, src, g_send.at[slot, idx], g_recv.at[slot, idx],
+                                            device_id=dev(YN if t == 1 else XN), device_id_type=MESH)
+
+    def relay(k, slot, cls, ph, t, fn):
+        n = 8 - ph
+        if n % 2 == 0:
+            fn(relay_copy(slot, cls, ph, n // 2, t))
+        else:
+            for par in (0, 1):
+                h = (n + par) // 2
+                if (h if t == 1 else n - h) > 0:
+                    @pl.when(rem(k, 2) == par)
+                    def _():
+                        fn(relay_copy(slot, cls, ph, h, t))
 
     def first_of(k, cls):
         return div(k - cls + 7, 8)
@@ -280,8 +323,8 @@
                         ls_copy(3, k, h).start()
 
             aslot = rem(k, NA)
-            ls0 = split3(ls_ref[rem(k, 8), 0])
-            ls1 = split3(ls_ref[rem(k, 8), 1])
+            ls0 = split3(ls_ref[rem(k, NP), 0])
+            ls1 = split3(ls_ref[rem(k, NP), 1])
             lane0 = pl.multiple_of(rem(k, 2) * NB, NB)
 
             def update(ph):
@@ -299,7 +342,11 @@
 
                 acc = dot6(lh_ref[slot_1, rows, :], ls1) + dot6(lh_ref[slot_2, rows, :], ls0)
                 s_ref[rows, :] = s_ref[rows, :] - (u_ref[div(k, 2), rows, pl.ds(lane0, NB)] + acc)
-            phases(k, me, update)
+            phases(k + 1, me, update)
+
+            @pl.when(jnp.logical_and(r != rem(k, 2), k + NA < NBLK))
+            def _():
+                pl.semaphore_signal(a_free, inc=1, device_id=dev(SIB), device_id_type=MESH)
 
             @pl.when(jnp.logical_and(nxt < NBLK, rem(nxt, 8) == me))
             def _():
@@ -322,7 +369,7 @@
         @pl.when(jnp.logical_and(nxt < NBLK, rem(nxt, 8) == me))
         def _():
             i_n = div(nxt, 8)
-            sl = rem(nxt, 8)
+            sl = rem(nxt, NP)
             rows_n = pl.ds(pl.multiple_of(i_n * NB, NB), NB)
 
             @pl.when(k < 0)
@@ -331,7 +378,7 @@
 
             @pl.when(k >= 0)
             def _():
-                xs = dot_nt(s_ref[rows_n, :], li_ref[rem(k0, 8)])
+                xs = dot_nt(s_ref[rows_n, :], li_ref[rem(k0, NP)])
                 ls_ref[sl, 1] = xs
                 for n in range(4):
                     ls_copy(n, nxt, 1).start()
@@ -342,12 +389,16 @@
                 li_copy(n, nxt).start()
             ri = lax.broadcasted_iota(jnp.int32, (NB, NB), 0)
             ci = lax.broadcasted_iota(jnp.int32, (NB, NB), 1)
-            lkk_ref[...] = jnp.where(ri >= ci, lt_ref[...].T, 0.0)
+            lkk_ref[sl] = jnp.where(ri >= ci, lt_ref[...].T, 0.0)
+            lk_copy(1, nxt).start()
+
+            @pl.when(r != c)
+            def _():
+                lk_copy(0, nxt).start()
 
         @pl.when(active)
         def _():
-            li = li_ref[rem(k, 8)]
-            lkk = lkk_ref[...]
+            li = li_ref[rem(k, NP)]
 
             li3 = split3(li)
 
@@ -357,18 +408,21 @@
                 x = dot6(parts_lhs(s_ref[rows, :]), li3)
                 g_ref[slot_k, me, ph:8] = x.reshape(8 - ph, NB, NB)
                 lh_ref[slot_k, rows, :] = parts_lhs(x)
-
-                @pl.when(8 * ph + me == k)
-                def _():
-                    g_ref[slot_k, me, ph] = lkk
-            phases(k, me, solve)
+            phases(k + 1, me, solve)
 
             @pl.when(jnp.logical_and(k + 2 < NBLK, rem(k + 2, 8) == me))
             def _():
-                ls_ref[rem(k + 2, 8), 0] = g_ref[slot_k, me, div(k + 2, 8)]
+                ls_ref[rem(k + 2, NP), 0] = g_ref[slot_k, me, div(k + 2, 8)]
                 for n in range(4):
                     ls_copy(n, k + 2, 0).start()
 
+            @pl.when(rem(k, 8) == me)
+            def _():
+                lk_copy(1, k).wait_send()
+
+                @pl.when(r != c)
+                def _():
+                    lk_copy(0, k).wait_send()
             for n in range(4):
                 sent = rem(k, 8) == me
                 if n == 3:
@@ -390,21 +444,23 @@
             def send(ph):
                 for t in range(3):
                     piece_copy(t, slot_k, me, ph, False).start()
-            phases(k, me, send)
+            phases(k + 3, me, send)
+
+            @pl.when(jnp.logical_and(jnp.logical_and(r == c, rem(k, 2) == c), rem(k, 8) != me))
+            def _():
+                lk_copy(0, k).wait_recv()
+            row_outs(k, lambda n: row_copy(n, k).start())
 
         @pl.when(jnp.logical_and(k >= 1, k <= NBLK))
         def _():
-            for t, to, odd in ((1, YN, 0), (2, XN, 1)):
+            for t in (1, 2):
                 cls = class_of(*partner(groups[t]))
 
                 def fwd(ph):
                     piece_copy(t, slot_1, cls, ph, False).wait_recv()
                     piece_copy(t, slot_1, cls, ph, True).start()
-
-                    @pl.when(rem(k - 1, 2) == odd)
-                    def _():
-                        relay_copy(slot_1, cls, ph, to).start()
-                phases(k - 1, cls, fwd)
+                    relay(k - 1, slot_1, cls, ph, t, lambda cp: cp.start())
+                phases(k + 2, cls, fwd)
 
         @pl.when(k >= 2)
         def _():
@@ -412,20 +468,21 @@
             dg_cls = class_of(*partner(DG))
 
             def fwd_dg(ph):
-                piece_copy(3, slot_2, dg_cls, ph, False).wait_recv()
+                for t in (1, 2):
+                    relay(m, slot_2, dg_cls, ph, t, lambda cp: cp.wait_recv())
                 piece_copy(3, slot_2, dg_cls, ph, True).start()
-            phases(m, dg_cls, fwd_dg)
+            phases(m + 3, dg_cls, fwd_dg)
 
             sib_cls = class_of(*partner(SIB))
-            phases(m, sib_cls, lambda ph: piece_copy(0, slot_2, sib_cls, ph, False).wait_recv())
+            phases(m + 3, sib_cls, lambda ph: piece_copy(0, slot_2, sib_cls, ph, False).wait_recv())
             for t in range(1, 4):
                 cls = class_of(*partner(xor_sib(groups[t])))
-                phases(m, cls, lambda ph: piece_copy(t, slot_2, cls, ph, True).wait_recv())
+                phases(m + 3, cls, lambda ph: piece_copy(t, slot_2, cls, ph, True).wait_recv())
 
             @pl.when(rem(m, 2) == c)
             def _():
                 for e in range(4):
-                    phases(m, 2 * e + r, lambda ph: out_copy(m, ph, e).start())
+                    phases(m + 3, 2 * e + r, lambda ph: out_copy(m, ph, e).start())
 
             start = div(m + 3, 2)
             for v in range(8):
@@ -453,30 +510,35 @@
             def finish(ph):
                 for t in range(3):
                     piece_copy(t, slot_2, me, ph, False).wait_send()
-            phases(m, me, finish)
+            phases(m + 3, me, finish)
             for t in range(1, 4):
                 cls = class_of(*partner(groups[t]))
 
                 def finish_fwd(ph):
                     piece_copy(t, slot_2, cls, ph, True).wait_send()
                     if t < 3:
-                        @pl.when(rem(m, 2) == t - 1)
-                        def _():
-                            relay_copy(slot_2, cls, ph, YN).wait_send()
-                phases(m, cls, finish_fwd)
+                        relay(m, slot_2, cls, ph, t, lambda cp: cp.wait_send())
+                phases(m + 3, cls, finish_fwd)
 
             @pl.when(rem(m, 2) == c)
             def _():
                 for e in range(4):
-                    phases(m, 2 * e + r, lambda ph: out_copy(m, ph, e).wait())
+                    phases(m + 3, 2 * e + r, lambda ph: out_copy(m, ph, e).wait())
 
             @pl.when(m + NSLOT < NBLK)
             def _():
                 for t in range(3):
                     pl.semaphore_signal(credit.at[t], inc=1, device_id=dev(groups[t]), device_id_type=MESH)
 
+        @pl.when(active)
+        def _():
+            row_outs(k, lambda n: row_copy(n, k).wait())
+
         @pl.when(k + 4 < NBLK)
         def _():
+            @pl.when(jnp.logical_and(k >= 2, rem(k0, 2) == r))
+            def _():
+                pl.semaphore_wait(a_free, 1)
             fetch(k + 4)
         return 0
 
@@ -499,22 +561,26 @@
                 pltpu.VMEM((NSLOT, 8, 8, NB, NB), F32),
                 pltpu.VMEM((NA, 8, NB, NB), F32),
                 pltpu.VMEM((1024, NB), F32),
-                pltpu.VMEM((8, 2, NB, NB), F32),
-                pltpu.VMEM((8, NB, NB), F32),
-                pltpu.VMEM((NB, NB), F32),
+                pltpu.VMEM((NP, 2, NB, NB), F32),
+                pltpu.VMEM((NP, NB, NB), F32),
+                pltpu.VMEM((NP, NB, NB), F32),
                 pltpu.VMEM((NB, NB), F32),
                 pltpu.VMEM((NB, NB), F32),
                 pltpu.VMEM((NSLOT, 1024, 384), BF16),
                 dma((3, 4)),
-                dma((8,)),
-                dma((8, 2)),
-                dma((NSLOT, 7)),
-                dma((NSLOT, 7)),
+                dma((NP,)),
+                dma((NP, 2)),
+                dma((NSLOT, 8)),
+                dma((NSLOT, 8)),
                 pltpu.SemaphoreType.REGULAR((3,)),
                 dma((NA,)),
                 dma((NA,)),
                 dma((NA,)),
                 dma((4,)),
+                dma((3,)),
+                dma((2,)),
+                dma((NP,)),
+                pltpu.SemaphoreType.REGULAR,
             ],
             compiler_params=pltpu.CompilerParams(
                 collective_id=0, has_side_effects=True, vmem_limit_bytes=67043328),

time: 859 us -> 775 us (0.902)
  Pallas kernels: 814 us -> 730 us
    pallas_call x1, Pallas kernels: 814 us -> 730 us  [local_factor(): pl.pallas_call(kernel, out_shape=jax.ShapeDtypeStruct((8, 4, 8, 4, NB, NB...]
where the time goes in v3:
time: 775 us
  Pallas kernels  730 us (94%)
  other arithmetic  45.2 us (6%)
    pallas_call x1, Pallas kernels, local_factor(): pl.pallas_call(kernel, out_shape=jax.ShapeDtypeStruct((8, 4, 8, 4, NB, NB...  730 us
    select_n x1, other arithmetic, local_factor(): return jnp.where(keep[:, :, None, None], fac, 0.0)  44.6 us

profile of v3, /device:TPU:0, one launch (start us, length us, event | category | flops | bytes accessed | tf_op | source)
XLA Modules:
  0.0 774.9 jit_solution(9051251881087208216)
XLA Ops:
  0.0 0.7 broadcast_compare_fusion
  0.7 729.7 %chol_all.1 = f32[8,4,8,4,128,128]{5,4,3,2,1,0:T(8,128)} custom-call(f32[8,4,8,4,128,128]{5,4,3,2,1,0:T(8,128)} %bitcast.a_ref), custom_call_target="tpu_custom_call" | custom-call | tf_op jit(solution)/shard_map/chol_all/pallas_call | solution.py:554
  730.4 44.6 %broadcast_select_fusion = f32[32,32,128,128]{3,2,1,0:T(8,128)} fusion(f32[32,32,128,128]{3,2,1,0:T(8,128)} %bitcast.1, pred[32,32]{1,0:T(8,128)(4,1)} %broadcast_compare_fusion), kind=kLoop, calls=%fused_computation | loop fusion | flops 16777216 | bytes 134218752 | tf_op jit(solution)/shard_map/jit(_where)/select_n | solution.py:593
  (1 shorter events, 0.0 us)

commit v4 on v3

--- a/solution.py
+++ b/solution.py
@@ -23,7 +23,7 @@
     rowi = lax.broadcasted_iota(jnp.int32, (8, 128), 0)
     lanei = lax.broadcasted_iota(jnp.int32, (8, 128), 1)
     for g in range(G):
-        z_ref[8*g:8*g+8, :] = jnp.where(lanei == rowi + 8*g, 1.0, 0.0).astype(jnp.float32)
+        z_ref[8*g:8*g+8, :] = jnp.where(lanei == rowi + 8*g, 1.0, 0.0).astype(F32)
     for g in range(G):
         rg = r_ref[8*g:8*g+8, :]
         zg = z_ref[8*g:8*g+8, :]
@@ -70,7 +70,7 @@
             zp = jnp.where(rowi == i, yz[i], zp)
         lt_ref[8*g:8*g+8, :] = yp
         z_ref[8*g:8*g+8, :] = zp
-        for r in range(g+1, G):
+        for r in range(g+1, min(G, g+1+2)):
             R = r_ref[8*r:8*r+8, :]
             cr = [bc(R[:, 8*g+j:8*g+j+1]) for j in range(8)]
             t = [cr[j]*w[j] for j in range(8)]
@@ -80,10 +80,15 @@
                 tz = [tz[i]+tz[i+1] for i in range(0, len(tz), 2)]
             r_ref[8*r:8*r+8, :] = R - t[0]
             z_ref[8*r:8*r+8, :] = z_ref[8*r:8*r+8, :] - tz[0]
-
-
-def dot_nt(a, b):
-    return lax.dot_general(a, b, (((1,), (1,)), ((), ())), precision=lax.Precision.HIGHEST, preferred_element_type=F32)
+        if g + 1 + 2 < G:
+            r0 = 8*(g+1+2)
+            s1, s2, s3 = split3(jnp.concatenate([yp, zp], axis=1))
+            rhs = jnp.concatenate([s1, s2, s1, s2, s3, s1], axis=0)
+            a1, a2, a3 = split3(yp)
+            lhs = jnp.concatenate([a1, a1, a2, a2, a1, a3], axis=0)
+            far = lax.dot_general(lhs, rhs, (((0,), (0,)), ((), ())), preferred_element_type=F32)
+            r_ref[r0:128, :] = r_ref[r0:128, :] - far[r0:128, 0:128]
+            z_ref[r0:128, :] = z_ref[r0:128, :] - far[r0:128, 128:256]
 
 
 def dot_bf(a, b):
@@ -356,7 +361,7 @@
                 p1 = g_ref[slot_1, me, i_n]
                 p2 = g_ref[slot_2, me, i_n]
                 d_ref[...] = (ac_ref[rem(nxt, NA), i_n] - u_ref[div(nxt, 2), rows_n, pl.ds(lane_n, NB)]
-                              - (dot_nt(p1, p1) + dot_nt(p2, p2)))
+                              - (dot6(parts_lhs(p1), split3(p1)) + dot6(parts_lhs(p2), split3(p2))))
 
             @pl.when(jnp.logical_not(own_k))
             def _():
@@ -378,11 +383,11 @@
 
             @pl.when(k >= 0)
             def _():
-                xs = dot_nt(s_ref[rows_n, :], li_ref[rem(k0, NP)])
+                xs = dot6(parts_lhs(s_ref[rows_n, :]), split3(li_ref[rem(k0, NP)]))
                 ls_ref[sl, 1] = xs
                 for n in range(4):
                     ls_copy(n, nxt, 1).start()
-                d_ref[...] = d_ref[...] - dot_nt(xs, xs)
+                d_ref[...] = d_ref[...] - dot6(parts_lhs(xs), split3(xs))
 
             cholinv(d_ref, li_ref.at[sl], lt_ref)
             for n in range(4):

time: 775 us -> 762 us (0.983)
  Pallas kernels: 730 us -> 716 us
    pallas_call x1, Pallas kernels: 730 us -> 716 us  [local_factor(): pl.pallas_call(kernel, out_shape=jax.ShapeDtypeStruct((8, 4, 8, 4, NB, NB...]
where the time goes in v4:
time: 762 us
  Pallas kernels  716 us (94%)
  other arithmetic  45.2 us (6%)
    pallas_call x1, Pallas kernels, local_factor(): pl.pallas_call(kernel, out_shape=jax.ShapeDtypeStruct((8, 4, 8, 4, NB, NB...  716 us
    select_n x1, other arithmetic, local_factor(): return jnp.where(keep[:, :, None, None], fac, 0.0)  44.6 us

profile of v4, /device:TPU:0, one launch (start us, length us, event | category | flops | bytes accessed | tf_op | source)
XLA Modules:
  0.0 761.6 jit_solution(2962926556682117712)
XLA Ops:
  0.0 0.7 broadcast_compare_fusion
  0.7 716.3 %chol_all.1 = f32[8,4,8,4,128,128]{5,4,3,2,1,0:T(8,128)} custom-call(f32[8,4,8,4,128,128]{5,4,3,2,1,0:T(8,128)} %bitcast.a_ref), custom_call_target="tpu_custom_call" | custom-call | tf_op jit(solution)/shard_map/chol_all/pallas_call | solution.py:559
  717.0 44.6 %broadcast_select_fusion = f32[32,32,128,128]{3,2,1,0:T(8,128)} fusion(f32[32,32,128,128]{3,2,1,0:T(8,128)} %bitcast.1, pred[32,32]{1,0:T(8,128)(4,1)} %broadcast_compare_fusion), kind=kLoop, calls=%fused_computation | loop fusion | flops 16777216 | bytes 134218752 | tf_op jit(solution)/shard_map/jit(_where)/select_n | solution.py:598
  (1 shorter events, 0.0 us)
